TPU v7x, 512 devices: a 8x2x16 block of a 8x8x16 slice. The times are simulated.
512 devices in a mesh: grp: 2 (over y), ctx: 32 (over z, core), hd: 8 (over x).
Axes of the slice: x: 8, y: 2, z: 16, core: 2. Of those that a mesh axis runs over, the one named last changes fastest.
The devices are a block of a 8x8x16 slice.
Arguments:
- query: bfloat16 [8192, 4096], P(('grp', 'ctx'), 'hd'), parts along dimension 0, may hold values from -6 to 6
- keys: bfloat16 [8192, 1024], P(('grp', 'ctx'), 'hd'), parts along dimension 0, may hold values from -6 to 6
- values: bfloat16 [8192, 1024], P(('grp', 'ctx'), 'hd'), parts along dimension 0, may hold values from -6 to 6
- m_x: bfloat16 [8192, 8192], P(('grp', 'ctx'), 'hd'), parts along dimension 0, may hold values from -6 to 6
- m_z: bfloat16 [8192, 8192], P(('grp', 'ctx'), 'hd'), parts along dimension 0, may hold values from -6 to 6
- m_b: bfloat16 [8192, 1024], P(('grp', 'ctx'), 'hd'), parts along dimension 0, may hold values from -6 to 6
- m_c: bfloat16 [8192, 1024], P(('grp', 'ctx'), 'hd'), parts along dimension 0, may hold values from -0.5 to 0.5
- dt_raw: bfloat16 [8192, 128], P(('grp', 'ctx'), 'hd'), parts along dimension 0, may hold values from -5 to 204
- dt_bias: float32 [128], P('hd'), may hold values from -0.5 to 0.5
- a_log: float32 [128], P('hd'), may hold values from -10 to 0
- d_skip: float32 [128], P('hd'), may hold values from 0.5 to 2
- norm_gain: float32 [8192], P('hd'), may hold values from 0.5 to 1.5
Outputs:
- context: bfloat16 [8192, 4096], P(('grp', 'ctx'), 'hd'), parts along dimension 0
- mixed: bfloat16 [8192, 8192], P(('grp', 'ctx'), 'hd'), parts along dimension 0
There are 2 independent parts, one for each index of `grp`. A program takes and returns all parts, laid end to end along the dimension named above; an argument that names none is the same for every part. Nothing has to cross between parts.
All inputs are finite; a program needn't handle non-finite values.
Results may differ from a plain program's by a relative error of at most 0.009.
Values may be sent and summed in bfloat16 or wider, within the bound.
No kernel may reach another device: no remote copies, remote signals or barrier semaphores. Data moves between devices by JAX's collectives and lax.ppermute only.
A program may use at most 64 MiB of HBM per device.

v0:
```python
import math
import jax
import jax.numpy as jnp
from jax import lax
from jax.sharding import Mesh
from jax.sharding import PartitionSpec as P

HEAD_SIZE = 128
MP = 64
MN = 128
CTX = ("ctx_0", "ctx_1")
GRP_CTX = ("grp", "ctx_0", "ctx_1")
norm_eps = 1e-05
masked_score = -1e30


def in_order(blocks, dim):
    blocks = jnp.moveaxis(blocks, 0, dim)
    shape = blocks.shape
    return blocks.reshape(*shape[:dim], shape[dim] * shape[dim + 1], *shape[dim + 2 :])


def stacked_from(shard, axes, order):
    blocks = shard
    for k in order:
        blocks = lax.all_gather(blocks, axes[k])
    done = order[::-1]
    back = [done.index(k) for k in range(len(axes))]
    blocks = blocks.transpose(*back, *range(len(axes), blocks.ndim))
    return blocks.reshape(-1, *shard.shape)


def gather_axes(shard, axes, order, dim):
    return in_order(stacked_from(shard, axes, order), dim)


def sent_together(arrays, axis, dim, along):
    ends, at = ([], 0)
    for a in arrays[:-1]:
        at += a.shape[along]
        ends.append(at)
    both = jnp.concatenate(arrays, axis=along)
    return tuple(jnp.split(lax.all_gather(both, axis, axis=dim, tiled=True), ends, axis=along))


def token_position(row_index, tok_rows, ctx_count):
    device = row_index // tok_rows
    within = row_index - device * tok_rows
    half_rows = tok_rows // 2
    second = within >= half_rows
    block_index = jnp.where(second, 2 * ctx_count - 1 - device, device)
    return block_index * half_rows + within - jnp.where(second, half_rows, 0)


def pick_block(total_rows, limit):
    selected = 1
    for candidate in range(1, min(total_rows, limit) + 1):
        if total_rows % candidate == 0:
            selected = candidate
    return selected


def folded_to_sequence(whole, ctx_count):
    half_rows = whole.shape[0] // (2 * ctx_count)
    blocks = whole.reshape((ctx_count, 2, half_rows) + whole.shape[1:])
    return jnp.concatenate([blocks[:, 0], blocks[::-1, 1]], axis=0).reshape(whole.shape)


def attend(query, keys, values):
    tok_rows = query.shape[0]
    ctx_count = lax.axis_size(CTX)
    kv_local = keys.shape[1] // HEAD_SIZE
    heads_per_group = query.shape[1] // keys.shape[1]
    query_heads = query.reshape(tok_rows, kv_local, heads_per_group, HEAD_SIZE)
    own_rows = lax.axis_index(CTX) * tok_rows + jnp.arange(tok_rows, dtype=jnp.int32)
    query_pos = token_position(own_rows, tok_rows, ctx_count)
    scaling = 1.0 / math.sqrt(HEAD_SIZE)
    start_max = jnp.full((kv_local, heads_per_group, tok_rows), masked_score, jnp.float32)
    start_sum = jnp.zeros((kv_local, heads_per_group, tok_rows), jnp.float32)
    start_acc = jnp.zeros((kv_local, heads_per_group, tok_rows, HEAD_SIZE), jnp.float32)
    start = jnp.int32(0)
    key_piece = gather_axes(keys, CTX, (0, 1), 0)
    value_piece = gather_axes(values, CTX, (0, 1), 0)
    piece_rows = key_piece.shape[0]
    rows_per_block = pick_block(piece_rows, 1024)

    def one_block(index, running):
        running_max, running_sum, running_acc = running
        offset = index * rows_per_block
        key_block = lax.dynamic_slice_in_dim(key_piece, offset, rows_per_block, 0).reshape(
            rows_per_block, kv_local, HEAD_SIZE
        )
        value_block = lax.dynamic_slice_in_dim(value_piece, offset, rows_per_block, 0).reshape(
            rows_per_block, kv_local, HEAD_SIZE
        )
        key_pos = token_position(
            start + offset + jnp.arange(rows_per_block, dtype=jnp.int32), tok_rows, ctx_count
        )
        visible = key_pos[None, :] <= query_pos[:, None]
        scores = (
            jnp.einsum("qhgd,khd->hgqk", query_heads, key_block, preferred_element_type=jnp.float32)
            * scaling
        )
        scores = jnp.where(visible, scores, masked_score)
        new_max = jnp.maximum(running_max, jnp.max(scores, axis=-1))
        weights = jnp.where(visible, jnp.exp(scores - new_max[..., None]), 0.0)
        factor = jnp.exp(running_max - new_max)
        new_sum = running_sum * factor + jnp.sum(weights, axis=-1)
        update = jnp.einsum(
            "hgqk,khd->hgqd",
            weights.astype(jnp.bfloat16),
            value_block,
            preferred_element_type=jnp.float32,
        )
        return (new_max, new_sum, running_acc * factor[..., None] + update)

    final_max, final_sum, final_acc = lax.fori_loop(
        0, piece_rows // rows_per_block, one_block, (start_max, start_sum, start_acc)
    )
    averaged = final_acc / final_sum[..., None]
    return jnp.transpose(averaged, (2, 0, 1, 3)).reshape(tok_rows, -1).astype(jnp.bfloat16)


def ssd_block(inputs, steps, rates, b_rows, c_rows):
    intersection = jnp.dot(c_rows, b_rows.T, preferred_element_type=jnp.float32)
    inputs = inputs.astype(jnp.float32)
    b_rows = b_rows.astype(jnp.float32)
    sequence_length = inputs.shape[0]
    running = jnp.cumsum(-steps * rates, axis=0)
    lower = jnp.arange(sequence_length)[:, None] >= jnp.arange(sequence_length)[None, :]
    spread = running[:, None, :] - running[None, :, :]
    decay = jnp.exp(jnp.where(lower[:, :, None], spread, -jnp.inf))
    weights = intersection[:, :, None] * decay * steps[None, :, :]
    inner = jnp.einsum("ijh,jhp->ihp", weights, inputs)
    tail_weight = jnp.exp(running[-1][None, :] - running) * steps
    state = jnp.einsum("jh,jhp,jn->hpn", tail_weight, inputs, b_rows)
    return (inner, state, jnp.exp(running[-1]), jnp.exp(running))


def chain_states(earlier, later):
    return (earlier[0] * later[0], earlier[1] * later[0][..., None, None] + later[1])


def ssd_sequence(inputs, steps, rates, b_rows, c_rows):
    sequence_length, head_count, width = inputs.shape
    block_len = math.gcd(sequence_length, 128)
    count = sequence_length // block_len
    c_blocks = c_rows.reshape(count, block_len, -1)
    inner, state, totals, scaled = jax.vmap(ssd_block, in_axes=(0, 0, None, 0, 0))(
        inputs.reshape(count, block_len, head_count, width),
        steps.reshape(count, block_len, head_count),
        rates,
        b_rows.reshape(count, block_len, -1),
        c_blocks,
    )
    running = lax.associative_scan(chain_states, (totals, state))
    entering = jnp.concatenate([jnp.zeros_like(running[1][:1]), running[1][:-1]], axis=0)
    carried = (
        jnp.einsum("cqn,chpn->cqhp", c_blocks.astype(jnp.float32), entering) * scaled[..., None]
    )
    return (inner + carried).reshape(sequence_length, head_count, width)


def gated_norm(gated_rows, norm_scale, group_count):
    row_count = gated_rows.shape[0]
    widened = (
        lax.optimization_barrier(gated_rows).astype(jnp.float32).reshape(row_count, group_count, -1)
    )
    power = jnp.mean(widened * widened, axis=-1, keepdims=True)
    return ((widened * lax.rsqrt(power + norm_eps)).reshape(row_count, -1) * norm_scale).astype(
        jnp.bfloat16
    )


def body(query, keys, values, m_x, m_z, m_b, m_c, dt_raw, dt_bias, a_log, d_skip, norm_gain):
    ctx_count = lax.axis_size(CTX)
    context_fold = attend(query, keys, values)
    groups_here = m_b.shape[1] // MN
    rates = jnp.exp(a_log)
    x_cols, z_cols, context_cols = (
        lax.all_to_all(m_x, CTX, split_axis=1, concat_axis=0, tiled=True),
        lax.all_to_all(m_z, CTX, split_axis=1, concat_axis=0, tiled=True),
        lax.all_to_all(context_fold, CTX, split_axis=1, concat_axis=0, tiled=True),
    )
    dt_whole, b_whole, c_whole = sent_together((dt_raw, m_b, m_c), CTX, 0, 1)
    x_cols = folded_to_sequence(x_cols, ctx_count)
    z_cols = folded_to_sequence(z_cols, ctx_count)
    context_cols = folded_to_sequence(context_cols, ctx_count)
    dt_whole = folded_to_sequence(dt_whole, ctx_count)
    b_whole = folded_to_sequence(b_whole, ctx_count)
    c_whole = folded_to_sequence(c_whole, ctx_count)
    sequence_length = x_cols.shape[0]
    width = x_cols.shape[1]
    sub_width = min(width, MP)
    head_count = width // sub_width
    first_head = lax.axis_index(CTX) * width // MP
    step_mine = jax.nn.softplus(
        lax.dynamic_slice_in_dim(dt_whole, first_head, head_count, 1).astype(jnp.float32)
        + lax.dynamic_slice_in_dim(dt_bias, first_head, head_count, 0)
    )
    rate_mine = lax.dynamic_slice_in_dim(rates, first_head, head_count, 0)
    skip_mine = lax.dynamic_slice_in_dim(d_skip, first_head, head_count, 0)
    x_mine = x_cols.reshape(sequence_length, head_count, sub_width)
    outputs = ssd_sequence(x_mine, step_mine, rate_mine, b_whole, c_whole)
    outputs = outputs + skip_mine[None, :, None] * x_mine.astype(jnp.float32)
    gated = (
        outputs.reshape(sequence_length, width) * jax.nn.silu(z_cols.astype(jnp.float32))
    ).astype(jnp.bfloat16)
    gated_rows, context = (
        lax.all_to_all(gated, CTX, split_axis=0, concat_axis=1, tiled=True),
        lax.all_to_all(context_cols, CTX, split_axis=0, concat_axis=1, tiled=True),
    )
    mixed = gated_norm(gated_rows, norm_gain, groups_here)
    return (context, mixed)


def solution(mesh):
    split = Mesh(
        mesh.devices.reshape(mesh.shape["grp"], 16, 2, mesh.shape["hd"]),
        ("grp", "ctx_0", "ctx_1", "hd"),
    )
    return jax.shard_map(
        body,
        mesh=split,
        in_specs=(
            P(GRP_CTX, "hd"),
            P(GRP_CTX, "hd"),
            P(GRP_CTX, "hd"),
            P(GRP_CTX, "hd"),
            P(GRP_CTX, "hd"),
            P(GRP_CTX, "hd"),
            P(GRP_CTX, "hd"),
            P(GRP_CTX, "hd"),
            P("hd"),
            P("hd"),
            P("hd"),
            P("hd"),
        ),
        out_specs=(P(GRP_CTX, "hd"), P(GRP_CTX, "hd")),
        check_vma=False,
    )
```

profile of v0, /device:TPU:65, one launch (start us, length us, event | category | flops | bytes accessed | tf_op | source)
XLA Modules:
  0.0 289.9 jit_solution(6494011130567231543)
XLA Ops:
  7.3 67.5 %all-gather = bf16[2048,128]{1,0:T(8,128)(2,1)} all-gather(bf16[128,128]{1,0:T(8,128)(2,1)} %param.15), channel_id=2, replica_groups=mesh['grp'=2,'ctx_0'=16,'ctx_1'=2,'hd'=8] {'ctx_0'}, dimensions={0}, use_global_device_ids=true | all-gather | bytes 557056 | tf_op jit(solution)/shard_map/all_gather | solution.py:26
  75.0 25.6 %all-gather.2 = bf16[2048,128]{1,0:T(8,128)(2,1)} all-gather(bf16[128,128]{1,0:T(8,128)(2,1)} %param.16), channel_id=4, replica_groups=mesh['grp'=2,'ctx_0'=16,'ctx_1'=2,'hd'=8] {'ctx_0'}, dimensions={0}, use_global_device_ids=true | all-gather | bytes 557056 | tf_op jit(solution)/shard_map/all_gather | solution.py:26
  101.5 18.2 %all-to-all-start.2 = ((bf16[128,32,32]{0,2,1:T(8,128)(2,1)}), bf16[128,32,32]{0,2,1:T(8,128)(2,1)S(1)}, u32[]{:S(2)}, u32[]{:S(2)}) async-start(bf16[128,32,32]{0,2,1:T(8,128)(2,1)} %bitcast.17), calls=%async_computation.2 | async-start | bytes 524288 | tf_op jit(solution)/shard_map/all_to_all | solution.py:181
  124.4 17.4 %all-to-all-done.2 = bf16[128,32,32]{0,2,1:T(8,128)(2,1)S(1)} async-done(((bf16[128,32,32]{0,2,1:T(8,128)(2,1)}), bf16[128,32,32]{0,2,1:T(8,128)(2,1)S(1)}, u32[]{:S(2)}, u32[]{:S(2)}) %all-to-all-start.2) | async-done | bytes 262176 | tf_op jit(solution)/shard_map/all_to_all | solution.py:181
  141.9 5.0 %all-to-all-start.3 = ((bf16[128,32,32]{0,2,1:T(8,128)(2,1)}), bf16[128,32,32]{0,2,1:T(8,128)(2,1)}, u32[]{:S(2)}, u32[]{:S(2)}) async-start(bf16[128,32,32]{0,2,1:T(8,128)(2,1)} %bitcast.54), calls=%async_computation.3 | async-start | bytes 524288 | tf_op jit(solution)/shard_map/all_to_all | solution.py:182
  151.3 2.4 copy.148
  153.7 16.5 %while.20 = (s32[]{:T(128)}, f32[1,4,128]{2,1,0:T(4,128)S(1)}, f32[1,4,128]{2,1,0:T(4,128)S(1)}, f32[1,4,128,128]{3,2,1,0:T(8,128)}, bf16[4096,128]{1,0:T(8,128)...) while((s32[]{:T(128)}, f32[1,4,128]{2,1,0:T(4,128)S(1)}, ...), condition=%wide.region_3.4_spmd.clone, body=%wide.region_0.3_spmd.clone.sunk | while | flops 275610752 | bytes 10134783 | solution.py:117
  155.3 1.8 fusion.98
  159.4 1.8 fusion.98
  163.6 1.8 fusion.98
  167.7 1.8 fusion.98
  172.0 12.6 %all-to-all-start = ((bf16[128,32,16]{0,2,1:T(8,128)(2,1)}), bf16[128,32,16]{0,2,1:T(8,128)(2,1)S(1)}, u32[]{:S(2)}, u32[]{:S(2)}) async-start(bf16[128,32,16]{0,2,1:T(8,128)(2,1)} %bitcast.11), calls=%async_computation | async-start | bytes 262144 | tf_op jit(solution)/shard_map/all_to_all | solution.py:183
  189.9 11.9 %all-to-all-done = bf16[128,32,16]{0,2,1:T(8,128)(2,1)S(1)} async-done(((bf16[128,32,16]{0,2,1:T(8,128)(2,1)}), bf16[128,32,16]{0,2,1:T(8,128)(2,1)S(1)}, u32[]{:S(2)}, u32[]{:S(2)}) %all-to-all-start) | async-done | bytes 131104 | tf_op jit(solution)/shard_map/all_to_all | solution.py:183
  203.5 5.5 %all-to-all-start.1 = ((bf16[32,128,16]{1,2,0:T(8,128)(2,1)}), bf16[32,128,16]{1,2,0:T(8,128)(2,1)}, u32[]{:S(2)}, u32[]{:S(2)}) async-start(bf16[32,128,16]{1,2,0:T(8,128)(2,1)} %copy.153), calls=%async_computation.1 | async-start | bytes 262144 | tf_op jit(solution)/shard_map/all_to_all | solution.py:211
  209.0 4.6 %all-gather.8.cloned.1.call-done = bf16[4096,272]{1,0:T(8,128)(2,1)} async-done(((bf16[128,272]{1,0:T(8,128)(2,1)}), bf16[4096,272]{1,0:T(8,128)(2,1)}) %all-gather.8.cloned.1.call-update) | async-done | bytes 2228240 | tf_op jit(solution)/shard_map/all_gather | solution.py:43
  218.0 2.9 copy.166
  220.8 1.8 fusion.77
  226.8 2.9 %fusion.71 = (bf16[4096,128]{1,0:T(8,128)(2,1)S(1)}, bf16[4096,128]{1,0:T(8,128)(2,1)S(1)}) fusion(bf16[4096,272]{1,0:T(8,128)(2,1)} %all-gather.8.cloned.1.call-done), kind=kLoop, calls=%fused_computation.137 | loop fusion | bytes 4194304 | tf_op jit(solution)/shard_map/split | solution.py:43
  238.1 5.8 %pad.103 = f32[32,1,32,128]{3,2,0,1:T(8,128)S(1)} pad(f32[16,1,32,128]{3,2,0,1:T(8,128)} %add.239, f32[]{:T(128)} %constant.191.clone.1), padding=1_0_1x0_0_0x0_0_0x0_0_0 | pad | bytes 786436
  245.0 3.5 %fusion.41 = f32[32,128,1,32]{1,3,0,2:T(8,128)} fusion(bf16[32,128,128]{2,1,0:T(8,128)(2,1)} %bitcast.209, bf16[32,128,128]{2,1,0:T(8,128)(2,1)S(1)} %bitcast.197, f32[32,128]{1,0:T(8,128)S(1)} %bitcast.228, f32[32,128]{1,0:T(8,128)S(1)} %bitcast.226, pred[128,128]{1,0:T(8,128)(4,1)S(1)} %copy-done.13, bf16[32,128,32]{1,0,2:T(8,128)(2,1)S(1)} %copy-done.1), kind=kOutput, calls=%fused_computation.63 | convolution fusion | flops 169869312 | bytes 2932736 | tf_op jit(solution)/shard_map/vmap(ijh,jhp->ihp)/dot_general | solution.py:134
  248.6 3.2 %fusion.48 = bf16[32,128,32]{1,2,0:T(8,128)(2,1)} fusion(f32[32,128,1,32]{1,3,0,2:T(8,128)} %fusion.41, bf16[32,128,128]{2,1,0:T(8,128)(2,1)S(1)} %bitcast.210, f32[32,128,32]{1,0,2:T(8,128)} %reshape.333, bf16[31,1,32,128]{3,2,0,1:T(8,128)(2,1)S(1)} %slice_add_fusion.5, f32[]{:T(128)} %bitcast.53, f32[32,128]{1,0:T(8,128)S(1)} %copy-done.14, ...), kind=kOutput, calls=%fused_computation.68 | convolution fusion | flops 34996224 | bytes 2891780 | tf_op jit(solution)/shard_map/cqn,chpn->cqhp/dot_general | solution.py:159
  251.8 8.3 %all-to-all-start.4 = ((bf16[32,128,32]{1,2,0:T(8,128)(2,1)}), bf16[32,128,32]{1,2,0:T(8,128)(2,1)S(1)}, u32[]{:S(2)}, u32[]{:S(2)}) async-start(bf16[32,128,32]{1,2,0:T(8,128)(2,1)} %fusion.48), calls=%async_computation.4 | async-start | bytes 524288 | tf_op jit(solution)/shard_map/all_to_all | solution.py:210
  260.1 1.7 copy.176
  261.8 20.4 %all-to-all-done.4 = bf16[32,128,32]{1,2,0:T(8,128)(2,1)S(1)} async-done(((bf16[32,128,32]{1,2,0:T(8,128)(2,1)}), bf16[32,128,32]{1,2,0:T(8,128)(2,1)S(1)}, u32[]{:S(2)}, u32[]{:S(2)}) %all-to-all-start.4) | async-done | bytes 262176 | tf_op jit(solution)/shard_map/all_to_all | solution.py:210
  (203 shorter events, 46.9 us)
Async XLA Ops:
  7.2 93.4 %copy-start.3 = (bf16[128,1024]{1,0:T(8,128)(2,1)S(1)}, bf16[128,1024]{1,0:T(8,128)(2,1)}, u32[]{:S(2)}) copy-start(bf16[128,1024]{1,0:T(8,128)(2,1)} %param.17) | copy-start | bytes 786436
  7.2 112.6 %copy-start.16 = (bf16[128,16]{0,1:T(8,128)(2,1)S(1)}, bf16[128,16]{0,1:T(8,128)(2,1)}, u32[]{:S(2)}) copy-start(bf16[128,16]{0,1:T(8,128)(2,1)} %param.21) | copy-start | bytes 12292
  7.2 112.8 %copy-start.11 = (bf16[128,128]{1,0:T(8,128)(2,1)S(1)}, bf16[128,128]{1,0:T(8,128)(2,1)}, u32[]{:S(2)}) copy-start(bf16[128,128]{1,0:T(8,128)(2,1)} %param.20) | copy-start | bytes 98308
  7.2 112.7 %copy-start.12 = (bf16[128,128]{1,0:T(8,128)(2,1)S(1)}, bf16[128,128]{1,0:T(8,128)(2,1)}, u32[]{:S(2)}) copy-start(bf16[128,128]{1,0:T(8,128)(2,1)} %param.19) | copy-start | bytes 98308
  7.2 113.6 %copy-start.7 = (bf16[128,512]{1,0:T(8,128)(2,1)S(1)}, bf16[128,512]{1,0:T(8,128)(2,1)}, u32[]{:S(2)}) copy-start(bf16[128,512]{1,0:T(8,128)(2,1)} %param.14) | copy-start | bytes 393220
  7.2 113.9 %copy-start.17 = (f32[16]{0:T(128)S(1)}, f32[16]{0:T(128)}, u32[]{:S(2)}) copy-start(f32[16]{0:T(128)} %param.23) | copy-start | bytes 196
  7.2 114.5 %copy-start.18 = (f32[16]{0:T(128)S(1)}, f32[16]{0:T(128)}, u32[]{:S(2)}) copy-start(f32[16]{0:T(128)} %param.22) | copy-start | bytes 196
  7.2 115.2 %copy-start.4 = (bf16[128,1024]{1,0:T(8,128)(2,1)S(1)}, bf16[128,1024]{1,0:T(8,128)(2,1)}, u32[]{:S(2)}) copy-start(bf16[128,1024]{1,0:T(8,128)(2,1)} %param.18) | copy-start | bytes 786436
  7.3 142.6 %all-gather.10.cloned.1.call-start = ((), (), s32[]{:S(2)}) async-start(), calls=%async_computation.6 | async-start | bytes 1572864 | tf_op jit(solution)/shard_map/all_gather | solution.py:26
  74.8 48.4 %copy-start.19 = (f32[16]{0:T(128)S(1)}, f32[16]{0:T(128)}, u32[]{:S(2)}) copy-start(f32[16]{0:T(128)} %param.24) | copy-start | bytes 196
  74.9 76.4 %all-gather.12.cloned.1.call-start = ((), (), s32[]{:S(2)}) async-start(), calls=%async_computation.7 | async-start | bytes 1572864 | tf_op jit(solution)/shard_map/all_gather | solution.py:26
  101.5 40.4 %all-to-all-start.2 = ((bf16[128,32,32]{0,2,1:T(8,128)(2,1)}), bf16[128,32,32]{0,2,1:T(8,128)(2,1)S(1)}, u32[]{:S(2)}, u32[]{:S(2)}) async-start(bf16[128,32,32]{0,2,1:T(8,128)(2,1)} %bitcast.17), calls=%async_computation.2 | async-start | bytes 524288 | tf_op jit(solution)/shard_map/all_to_all | solution.py:181
  119.7 93.9 %all-gather.8.cloned.1.call-start = ((), (), s32[]{:S(2)}) async-start(), calls=%async_computation.5 | async-start | bytes 3244032 | tf_op jit(solution)/shard_map/all_gather | solution.py:43
  141.9 30.1 %all-to-all-start.3 = ((bf16[128,32,32]{0,2,1:T(8,128)(2,1)}), bf16[128,32,32]{0,2,1:T(8,128)(2,1)}, u32[]{:S(2)}, u32[]{:S(2)}) async-start(bf16[128,32,32]{0,2,1:T(8,128)(2,1)} %bitcast.54), calls=%async_computation.3 | async-start | bytes 524288 | tf_op jit(solution)/shard_map/all_to_all | solution.py:182
  172.0 29.9 %all-to-all-start = ((bf16[128,32,16]{0,2,1:T(8,128)(2,1)}), bf16[128,32,16]{0,2,1:T(8,128)(2,1)S(1)}, u32[]{:S(2)}, u32[]{:S(2)}) async-start(bf16[128,32,16]{0,2,1:T(8,128)(2,1)} %bitcast.11), calls=%async_computation | async-start | bytes 262144 | tf_op jit(solution)/shard_map/all_to_all | solution.py:183
  186.0 44.7 %copy-start = (bf16[32,128,32]{1,0,2:T(8,128)(2,1)}, bf16[32,128,32]{1,0,2:T(8,128)(2,1)S(1)}, u32[]{:S(2)}) copy-start(bf16[32,128,32]{1,0,2:T(8,128)(2,1)S(1)} %reshape.325) | copy-start | bytes 786436
  203.5 48.3 %all-to-all-start.1 = ((bf16[32,128,16]{1,2,0:T(8,128)(2,1)}), bf16[32,128,16]{1,2,0:T(8,128)(2,1)}, u32[]{:S(2)}, u32[]{:S(2)}) async-start(bf16[32,128,16]{1,2,0:T(8,128)(2,1)} %copy.153), calls=%async_computation.1 | async-start | bytes 262144 | tf_op jit(solution)/shard_map/all_to_all | solution.py:211
  218.0 12.2 %copy-start.9 = (f32[4096,1]{0,1:T(1,128)}, f32[4096,1]{0,1:T(1,128)S(1)}, u32[]{:S(2)}) copy-start(f32[4096,1]{0,1:T(1,128)S(1)} %get-tuple-element.305) | copy-start | bytes 49156
  237.9 7.1 %copy-start.1 = (bf16[32,128,32]{1,0,2:T(8,128)(2,1)S(1)}, bf16[32,128,32]{1,0,2:T(8,128)(2,1)}, u32[]{:S(2)}) copy-start(bf16[32,128,32]{1,0,2:T(8,128)(2,1)} %copy-done) | copy-start | bytes 786436
  237.9 7.1 %copy-start.10 = (f32[4096,1]{0,1:T(1,128)S(1)}, f32[4096,1]{0,1:T(1,128)}, u32[]{:S(2)}) copy-start(f32[4096,1]{0,1:T(1,128)} %copy-done.9) | copy-start | bytes 49156
  237.9 7.1 %copy-start.13 = (pred[128,128]{1,0:T(8,128)(4,1)S(1)}, pred[128,128]{1,0:T(8,128)(4,1)}, u32[]{:S(2)}) copy-start(pred[128,128]{1,0:T(8,128)(4,1)} %iota_compare_fusion) | copy-start | bytes 49156
  245.0 3.6 %copy-start.14 = (f32[32,128]{1,0:T(8,128)S(1)}, f32[32,128]{1,0:T(8,128)}, u32[]{:S(2)}) copy-start(f32[32,128]{1,0:T(8,128)} %get-tuple-element.326) | copy-start | bytes 49156
  248.6 33.9 %copy-start.15 = (f32[1024]{0:T(1024)S(1)}, f32[1024]{0:T(1024)}, u32[]{:S(2)}) copy-start(f32[1024]{0:T(1024)} %param.25) | copy-start | bytes 12292
  251.8 30.4 %all-to-all-start.4 = ((bf16[32,128,32]{1,2,0:T(8,128)(2,1)}), bf16[32,128,32]{1,2,0:T(8,128)(2,1)S(1)}, u32[]{:S(2)}, u32[]{:S(2)}) async-start(bf16[32,128,32]{1,2,0:T(8,128)(2,1)} %fusion.48), calls=%async_computation.4 | async-start | bytes 524288 | tf_op jit(solution)/shard_map/all_to_all | solution.py:210
  (11 other events, 14.5 us)
Sparse Core Ops, SparseCore 0:
  75.0 23.9 all-gather.9
  101.1 30.5 all-gather.11
  133.9 79.7 all-gather.7
where the time goes:
time: 292 us; the launch traced here: 290 us
  blocking collectives  93.1 us (32%)
  waiting for transfers between devices  54.5 us (19%)
  starting transfers between devices  49.8 us (17%)
  local copies, waits for them, and re-layouts  44.6 us (15%)
  other arithmetic  17.3 us (6%)
  matrix products  15.8 us (5%)
  between operations  14.5 us (5%)
    all_gather x2, blocking collectives, stacked_from(): blocks = lax.all_gather(blocks, axes[k])  93.1 us
    all_to_all x1, waiting for transfers between devices, body(): lax.all_to_all(gated, CTX, split_axis=0, concat_axis=1, tiled=True)  20.4 us
    all_to_all x1, starting transfers between devices, body(): lax.all_to_all(m_x, CTX, split_axis=1, concat_axis=0, tiled=True)  18.2 us
    all_to_all x1, waiting for transfers between devices, body(): lax.all_to_all(m_x, CTX, split_axis=1, concat_axis=0, tiled=True)  17.4 us
    all_to_all x1, starting transfers between devices, body(): lax.all_to_all(context_fold, CTX, split_axis=1, concat_axis=0, tiled=True)  12.6 us
    unnamed x50, local copies, waits for them, and re-layouts  12.3 us
    all_to_all x1, waiting for transfers between devices, body(): lax.all_to_all(context_fold, CTX, split_axis=1, concat_axis=0, tiled=True)  11.9 us
    all_to_all x1, starting transfers between devices, body(): lax.all_to_all(gated, CTX, split_axis=0, concat_axis=1, tiled=True)  8.33 us
  transfers between devices with their start and end apart: 8, of which 4 were waited for; matrix products, arithmetic and copies ran while one was open for 24% of the time, Pallas kernels for 0%

commit v1 on v0

--- a/solution.py
+++ b/solution.py
@@ -178,7 +178,9 @@
     groups_here = m_b.shape[1] // MN
     rates = jnp.exp(a_log)
     x_cols, z_cols, context_cols = (
-        lax.all_to_all(m_x, CTX, split_axis=1, concat_axis=0, tiled=True),
+        jnp.concatenate(
+            lax.all_to_all(jnp.stack(jnp.split(m_x, lax.axis_size(CTX), axis=1)), CTX, 0, 0), axis=0
+        ),
         lax.all_to_all(m_z, CTX, split_axis=1, concat_axis=0, tiled=True),
         lax.all_to_all(context_fold, CTX, split_axis=1, concat_axis=0, tiled=True),
     )

time: 292 us -> 313 us (1.072)
  local copies, waits for them, and re-layouts: 44.6 us -> 66 us
  starting transfers between devices: 49.8 us -> 54.4 us
  waiting for transfers between devices: 54.5 us -> 50 us
    unnamed x50 -> x112, local copies, waits for them, and re-layouts: 12.3 us -> 32.7 us
    all_gather x1, waiting for transfers between devices: 4.58 us -> 0.02 us  [sent_together(): lax.all_gather(both, axis, axis=dim, tiled=True)]
    all_to_all x1, starting transfers between devices: 8.33 us -> 12.7 us  [body(): lax.all_to_all(gated, CTX, split_axis=0, concat_axis=1, tiled=True)]
  transfers between devices with their start and end apart: 8 -> 8, of which waited for: 4 -> 3; matrix products, arithmetic and copies ran while one was open for 24% -> 30% of each run, Pallas kernels for 0% -> 0%
where the time goes in v1:
time: 313 us; the launch traced here: 311 us
  blocking collectives  93 us (30%)
  local copies, waits for them, and re-layouts  66 us (21%)
  starting transfers between devices  54.4 us (17%)
  waiting for transfers between devices  50 us (16%)
  other arithmetic  17.3 us (6%)
  matrix products  15.9 us (5%)
  between operations  14.6 us (5%)
    all_gather x2, blocking collectives, stacked_from(): blocks = lax.all_gather(blocks, axes[k])  93 us
    unnamed x112, local copies, waits for them, and re-layouts  32.7 us
    all_to_all x1, waiting for transfers between devices, body(): lax.all_to_all(gated, CTX, split_axis=0, concat_axis=1, tiled=True)  20.4 us
    all_to_all x1, starting transfers between devices, body(): lax.all_to_all(jnp.stack(jnp.split(m_x, lax.axis_size(CTX), axis=1)), CTX...  18.2 us
    all_to_all x1, waiting for transfers between devices, body(): lax.all_to_all(jnp.stack(jnp.split(m_x, lax.axis_size(CTX), axis=1)), CTX...  17.4 us
    all_to_all x1, starting transfers between devices, body(): lax.all_to_all(context_fold, CTX, split_axis=1, concat_axis=0, tiled=True)  12.7 us
    all_to_all x1, starting transfers between devices, body(): lax.all_to_all(gated, CTX, split_axis=0, concat_axis=1, tiled=True)  12.7 us
    all_to_all x1, waiting for transfers between devices, body(): lax.all_to_all(context_fold, CTX, split_axis=1, concat_axis=0, tiled=True)  12 us
  transfers between devices with their start and end apart: 8, of which 3 were waited for; matrix products, arithmetic and copies ran while one was open for 30% of the time, Pallas kernels for 0%

profile of v1, /device:TPU:65, one launch (start us, length us, event | category | flops | bytes accessed | tf_op | source)
XLA Modules:
  0.0 311.5 jit_solution(3465666563560162243)
XLA Ops:
  7.3 67.4 %all-gather = bf16[2048,128]{1,0:T(8,128)(2,1)} all-gather(bf16[128,128]{1,0:T(8,128)(2,1)} %param.15), channel_id=2, replica_groups=mesh['grp'=2,'ctx_0'=16,'ctx_1'=2,'hd'=8] {'ctx_0'}, dimensions={0}, use_global_device_ids=true | all-gather | bytes 557056 | tf_op jit(solution)/shard_map/all_gather | solution.py:26
  74.8 25.6 %all-gather.2 = bf16[2048,128]{1,0:T(8,128)(2,1)} all-gather(bf16[128,128]{1,0:T(8,128)(2,1)} %param.16), channel_id=4, replica_groups=mesh['grp'=2,'ctx_0'=16,'ctx_1'=2,'hd'=8] {'ctx_0'}, dimensions={0}, use_global_device_ids=true | all-gather | bytes 557056 | tf_op jit(solution)/shard_map/all_gather | solution.py:26
  122.8 18.2 %all-to-all-start.2 = ((bf16[32,128,32]{1,2,0:T(8,128)(2,1)}), bf16[32,128,32]{1,2,0:T(8,128)(2,1)S(1)}, u32[]{:S(2)}, u32[]{:S(2)}) async-start(bf16[32,128,32]{1,2,0:T(8,128)(2,1)} %constant_dynamic-update-slice_fusion), calls=%async_computation.2 | async-start | bytes 524288 | tf_op jit(solution)/shard_map/all_to_all | solution.py:182
  145.8 17.4 %all-to-all-done.2 = bf16[32,128,32]{1,2,0:T(8,128)(2,1)S(1)} async-done(((bf16[32,128,32]{1,2,0:T(8,128)(2,1)}), bf16[32,128,32]{1,2,0:T(8,128)(2,1)S(1)}, u32[]{:S(2)}, u32[]{:S(2)}) %all-to-all-start.2) | async-done | bytes 262176 | tf_op jit(solution)/shard_map/all_to_all | solution.py:182
  163.2 4.9 %all-to-all-start.3 = ((bf16[128,32,32]{0,2,1:T(8,128)(2,1)}), bf16[128,32,32]{0,2,1:T(8,128)(2,1)}, u32[]{:S(2)}, u32[]{:S(2)}) async-start(bf16[128,32,32]{0,2,1:T(8,128)(2,1)} %bitcast.84), calls=%async_computation.3 | async-start | bytes 524288 | tf_op jit(solution)/shard_map/all_to_all | solution.py:184
  172.6 2.4 copy.209
  174.9 16.5 %while.20 = (s32[]{:T(128)}, f32[1,4,128]{2,1,0:T(4,128)S(1)}, f32[1,4,128]{2,1,0:T(4,128)S(1)}, f32[1,4,128,128]{3,2,1,0:T(8,128)}, bf16[4096,128]{1,0:T(8,128)...) while((s32[]{:T(128)}, f32[1,4,128]{2,1,0:T(4,128)S(1)}, ...), condition=%wide.region_3.4_spmd.clone, body=%wide.region_0.3_spmd.clone.sunk | while | flops 275610752 | bytes 10134783 | solution.py:117
  176.6 1.8 fusion.100
  180.7 1.8 fusion.100
  184.9 1.8 fusion.100
  189.0 1.8 fusion.100
  193.2 12.7 %all-to-all-start = ((bf16[128,32,16]{0,2,1:T(8,128)(2,1)}), bf16[128,32,16]{0,2,1:T(8,128)(2,1)S(1)}, u32[]{:S(2)}, u32[]{:S(2)}) async-start(bf16[128,32,16]{0,2,1:T(8,128)(2,1)} %bitcast.11), calls=%async_computation | async-start | bytes 262144 | tf_op jit(solution)/shard_map/all_to_all | solution.py:185
  211.3 12.0 %all-to-all-done = bf16[128,32,16]{0,2,1:T(8,128)(2,1)S(1)} async-done(((bf16[128,32,16]{0,2,1:T(8,128)(2,1)}), bf16[128,32,16]{0,2,1:T(8,128)(2,1)S(1)}, u32[]{:S(2)}, u32[]{:S(2)}) %all-to-all-start) | async-done | bytes 131104 | tf_op jit(solution)/shard_map/all_to_all | solution.py:185
  225.0 5.6 %all-to-all-start.1 = ((bf16[32,128,16]{1,2,0:T(8,128)(2,1)}), bf16[32,128,16]{1,2,0:T(8,128)(2,1)}, u32[]{:S(2)}, u32[]{:S(2)}) async-start(bf16[32,128,16]{1,2,0:T(8,128)(2,1)} %copy.214), calls=%async_computation.1 | async-start | bytes 262144 | tf_op jit(solution)/shard_map/all_to_all | solution.py:213
  233.5 1.4 negate_multiply_fusion
  234.9 2.9 copy.258
  237.7 1.8 fusion.79
  243.7 2.9 fusion.71
  255.2 5.8 %pad.103 = f32[32,1,32,128]{3,2,0,1:T(8,128)S(1)} pad(f32[16,1,32,128]{3,2,0,1:T(8,128)} %add.239, f32[]{:T(128)} %constant.191.clone.1), padding=1_0_1x0_0_0x0_0_0x0_0_0 | pad | bytes 786436
  262.1 3.5 %fusion.41 = f32[32,128,1,32]{1,3,0,2:T(8,128)} fusion(bf16[32,128,128]{2,1,0:T(8,128)(2,1)} %bitcast.270, bf16[32,128,128]{2,1,0:T(8,128)(2,1)S(1)} %bitcast.259, f32[32,128]{1,0:T(8,128)S(1)} %bitcast.289, f32[32,128]{1,0:T(8,128)S(1)} %bitcast.287, pred[128,128]{1,0:T(8,128)(4,1)S(1)} %copy-done.13, bf16[32,128,32]{1,0,2:T(8,128)(2,1)S(1)} %copy-done.2), kind=kOutput, calls=%fused_computation.63 | convolution fusion | flops 169869312 | bytes 2932736 | tf_op jit(solution)/shard_map/vmap(ijh,jhp->ihp)/dot_general | solution.py:134
  265.7 3.3 %fusion.48 = bf16[32,128,32]{1,2,0:T(8,128)(2,1)} fusion(f32[32,128,1,32]{1,3,0,2:T(8,128)} %fusion.41, bf16[32,128,128]{2,1,0:T(8,128)(2,1)S(1)} %bitcast.271, f32[32,128,32]{1,0,2:T(8,128)} %reshape.325, bf16[31,1,32,128]{3,2,0,1:T(8,128)(2,1)S(1)} %slice_add_fusion.5, f32[]{:T(128)} %bitcast.83, f32[32,128]{1,0:T(8,128)S(1)} %copy-done.14, ...), kind=kOutput, calls=%fused_computation.68 | convolution fusion | flops 34996224 | bytes 2891780 | tf_op jit(solution)/shard_map/cqn,chpn->cqhp/dot_general | solution.py:159
  269.0 12.7 %all-to-all-start.4 = ((bf16[32,128,32]{1,2,0:T(8,128)(2,1)}), bf16[32,128,32]{1,2,0:T(8,128)(2,1)S(1)}, u32[]{:S(2)}, u32[]{:S(2)}) async-start(bf16[32,128,32]{1,2,0:T(8,128)(2,1)} %fusion.48), calls=%async_computation.4 | async-start | bytes 524288 | tf_op jit(solution)/shard_map/all_to_all | solution.py:212
  281.7 1.7 copy.268
  283.4 20.4 %all-to-all-done.4 = bf16[32,128,32]{1,2,0:T(8,128)(2,1)S(1)} async-done(((bf16[32,128,32]{1,2,0:T(8,128)(2,1)}), bf16[32,128,32]{1,2,0:T(8,128)(2,1)S(1)}, u32[]{:S(2)}, u32[]{:S(2)}) %all-to-all-start.4) | async-done | bytes 262176 | tf_op jit(solution)/shard_map/all_to_all | solution.py:212
  (268 shorter events, 67.2 us)
Async XLA Ops:
  7.2 93.2 %copy-start = (bf16[128,1024]{1,0:T(8,128)(2,1)S(1)}, bf16[128,1024]{1,0:T(8,128)(2,1)}, u32[]{:S(2)}) copy-start(bf16[128,1024]{1,0:T(8,128)(2,1)} %param.17) | copy-start | bytes 786436
  7.2 164.1 %all-gather.10.cloned.1.call-start = ((), (), s32[]{:S(2)}) async-start(), calls=%async_computation.6 | async-start | bytes 1572864 | tf_op jit(solution)/shard_map/all_gather | solution.py:26
  74.7 97.9 %all-gather.12.cloned.1.call-start = ((), (), s32[]{:S(2)}) async-start(), calls=%async_computation.7 | async-start | bytes 1572864 | tf_op jit(solution)/shard_map/all_gather | solution.py:26
  100.4 40.7 %copy-start.16 = (bf16[128,16]{0,1:T(8,128)(2,1)S(1)}, bf16[128,16]{0,1:T(8,128)(2,1)}, u32[]{:S(2)}) copy-start(bf16[128,16]{0,1:T(8,128)(2,1)} %param.21) | copy-start | bytes 12292
  100.4 40.9 %copy-start.11 = (bf16[128,128]{1,0:T(8,128)(2,1)S(1)}, bf16[128,128]{1,0:T(8,128)(2,1)}, u32[]{:S(2)}) copy-start(bf16[128,128]{1,0:T(8,128)(2,1)} %param.20) | copy-start | bytes 98308
  100.5 40.8 %copy-start.12 = (bf16[128,128]{1,0:T(8,128)(2,1)S(1)}, bf16[128,128]{1,0:T(8,128)(2,1)}, u32[]{:S(2)}) copy-start(bf16[128,128]{1,0:T(8,128)(2,1)} %param.19) | copy-start | bytes 98308
  100.6 41.5 %copy-start.7 = (bf16[128,512]{1,0:T(8,128)(2,1)S(1)}, bf16[128,512]{1,0:T(8,128)(2,1)}, u32[]{:S(2)}) copy-start(bf16[128,512]{1,0:T(8,128)(2,1)} %param.14) | copy-start | bytes 393220
  100.6 41.8 %copy-start.17 = (f32[16]{0:T(128)S(1)}, f32[16]{0:T(128)}, u32[]{:S(2)}) copy-start(f32[16]{0:T(128)} %param.23) | copy-start | bytes 196
  100.7 42.4 %copy-start.18 = (f32[16]{0:T(128)S(1)}, f32[16]{0:T(128)}, u32[]{:S(2)}) copy-start(f32[16]{0:T(128)} %param.22) | copy-start | bytes 196
  100.7 43.1 %copy-start.4 = (bf16[128,1024]{1,0:T(8,128)(2,1)S(1)}, bf16[128,1024]{1,0:T(8,128)(2,1)}, u32[]{:S(2)}) copy-start(bf16[128,1024]{1,0:T(8,128)(2,1)} %param.18) | copy-start | bytes 786436
  100.9 43.7 %copy-start.19 = (f32[16]{0:T(128)S(1)}, f32[16]{0:T(128)}, u32[]{:S(2)}) copy-start(f32[16]{0:T(128)} %param.24) | copy-start | bytes 196
  122.8 40.4 %all-to-all-start.2 = ((bf16[32,128,32]{1,2,0:T(8,128)(2,1)}), bf16[32,128,32]{1,2,0:T(8,128)(2,1)S(1)}, u32[]{:S(2)}, u32[]{:S(2)}) async-start(bf16[32,128,32]{1,2,0:T(8,128)(2,1)} %constant_dynamic-update-slice_fusion), calls=%async_computation.2 | async-start | bytes 524288 | tf_op jit(solution)/shard_map/all_to_all | solution.py:182
  141.1 89.5 %all-gather.8.cloned.1.call-start = ((), (), s32[]{:S(2)}) async-start(), calls=%async_computation.5 | async-start | bytes 3244032 | tf_op jit(solution)/shard_map/all_gather | solution.py:43
  163.2 30.0 %all-to-all-start.3 = ((bf16[128,32,32]{0,2,1:T(8,128)(2,1)}), bf16[128,32,32]{0,2,1:T(8,128)(2,1)}, u32[]{:S(2)}, u32[]{:S(2)}) async-start(bf16[128,32,32]{0,2,1:T(8,128)(2,1)} %bitcast.84), calls=%async_computation.3 | async-start | bytes 524288 | tf_op jit(solution)/shard_map/all_to_all | solution.py:184
  193.2 30.0 %all-to-all-start = ((bf16[128,32,16]{0,2,1:T(8,128)(2,1)}), bf16[128,32,16]{0,2,1:T(8,128)(2,1)S(1)}, u32[]{:S(2)}, u32[]{:S(2)}) async-start(bf16[128,32,16]{0,2,1:T(8,128)(2,1)} %bitcast.11), calls=%async_computation | async-start | bytes 262144 | tf_op jit(solution)/shard_map/all_to_all | solution.py:185
  207.4 40.3 %copy-start.1 = (bf16[32,128,32]{1,0,2:T(8,128)(2,1)}, bf16[32,128,32]{1,0,2:T(8,128)(2,1)S(1)}, u32[]{:S(2)}) copy-start(bf16[32,128,32]{1,0,2:T(8,128)(2,1)S(1)} %reshape.317) | copy-start | bytes 786436
  225.0 44.0 %all-to-all-start.1 = ((bf16[32,128,16]{1,2,0:T(8,128)(2,1)}), bf16[32,128,16]{1,2,0:T(8,128)(2,1)}, u32[]{:S(2)}, u32[]{:S(2)}) async-start(bf16[32,128,16]{1,2,0:T(8,128)(2,1)} %copy.214), calls=%async_computation.1 | async-start | bytes 262144 | tf_op jit(solution)/shard_map/all_to_all | solution.py:213
  234.8 12.2 %copy-start.9 = (f32[4096,1]{0,1:T(1,128)}, f32[4096,1]{0,1:T(1,128)S(1)}, u32[]{:S(2)}) copy-start(f32[4096,1]{0,1:T(1,128)S(1)} %get-tuple-element.305) | copy-start | bytes 49156
  255.0 7.1 %copy-start.2 = (bf16[32,128,32]{1,0,2:T(8,128)(2,1)S(1)}, bf16[32,128,32]{1,0,2:T(8,128)(2,1)}, u32[]{:S(2)}) copy-start(bf16[32,128,32]{1,0,2:T(8,128)(2,1)} %copy-done.1) | copy-start | bytes 786436
  255.0 7.1 %copy-start.10 = (f32[4096,1]{0,1:T(1,128)S(1)}, f32[4096,1]{0,1:T(1,128)}, u32[]{:S(2)}) copy-start(f32[4096,1]{0,1:T(1,128)} %copy-done.9) | copy-start | bytes 49156
  255.0 7.1 %copy-start.13 = (pred[128,128]{1,0:T(8,128)(4,1)S(1)}, pred[128,128]{1,0:T(8,128)(4,1)}, u32[]{:S(2)}) copy-start(pred[128,128]{1,0:T(8,128)(4,1)} %iota_compare_fusion) | copy-start | bytes 49156
  262.1 3.6 %copy-start.14 = (f32[32,128]{1,0:T(8,128)S(1)}, f32[32,128]{1,0:T(8,128)}, u32[]{:S(2)}) copy-start(f32[32,128]{1,0:T(8,128)} %get-tuple-element.358) | copy-start | bytes 49156
  265.7 38.4 %copy-start.15 = (f32[1024]{0:T(1024)S(1)}, f32[1024]{0:T(1024)}, u32[]{:S(2)}) copy-start(f32[1024]{0:T(1024)} %param.25) | copy-start | bytes 12292
  269.0 34.8 %all-to-all-start.4 = ((bf16[32,128,32]{1,2,0:T(8,128)(2,1)}), bf16[32,128,32]{1,2,0:T(8,128)(2,1)S(1)}, u32[]{:S(2)}, u32[]{:S(2)}) async-start(bf16[32,128,32]{1,2,0:T(8,128)(2,1)} %fusion.48), calls=%async_computation.4 | async-start | bytes 524288 | tf_op jit(solution)/shard_map/all_to_all | solution.py:212
  (11 other events, 14.5 us)
Sparse Core Ops, SparseCore 0:
  74.8 23.9 all-gather.9
  100.9 30.5 all-gather.11
  144.1 84.2 all-gather.7
